TPU v7x, 32 devices: a whole 2x2x4 slice. The times are simulated.
32 devices in a mesh: pr: 8 (over y, x, core), pc: 4 (over z).
Axes of the slice: x: 2, y: 2, z: 4, core: 2. Of those that a mesh axis runs over, the one named last changes fastest.
Arguments:
- pair_array: bfloat16 [256, 256, 128], P('pr', 'pc'), may hold values from -6 to 6
- left_weight: bfloat16 [128, 128], replicated, may hold values from -0.5 to 0.5
- right_weight: bfloat16 [128, 128], replicated, may hold values from -0.5 to 0.5
- left_gate: bfloat16 [128, 128], replicated, may hold values from -0.5 to 0.5
- right_gate: bfloat16 [128, 128], replicated, may hold values from -0.5 to 0.5
- mid_gain: float32 [128], replicated, may hold values from 0.25 to 1.75
- out_weight: bfloat16 [128, 128], replicated, may hold values from -0.5 to 0.5
- out_gate: bfloat16 [128, 128], replicated, may hold values from -0.5 to 0.5
Outputs:
- pair_update: bfloat16 [256, 256, 128], P('pr', 'pc')
All inputs are finite; a program needn't handle non-finite values.
Results may differ from a plain program's by a relative error of at most 0.012.
Values may be sent and summed in bfloat16 or wider, within the bound.
A program may use at most 128 MiB of HBM per device.

v0:
```python
import jax
import jax.numpy as jnp
from jax import lax
from jax.sharding import PartitionSpec as P


def unit_channels(values, channel_gain):
    centred = values - jnp.mean(values, axis=-1, keepdims=True)
    return (
        centred
        * lax.rsqrt(jnp.mean(centred * centred, axis=-1, keepdims=True) + 1e-05)
        * channel_gain
    )


def make_factors(pair_in, left_weight, right_weight, left_gate, right_gate):
    left = jnp.einsum("ijc,cd->ijd", pair_in, left_weight, preferred_element_type=jnp.float32)
    left = left * jax.nn.sigmoid(
        jnp.einsum("ijc,cd->ijd", pair_in, left_gate, preferred_element_type=jnp.float32)
    )
    right = jnp.einsum("ijc,cd->ijd", pair_in, right_weight, preferred_element_type=jnp.float32)
    right = right * jax.nn.sigmoid(
        jnp.einsum("ijc,cd->ijd", pair_in, right_gate, preferred_element_type=jnp.float32)
    )
    return (pair_in, left.astype(jnp.bfloat16), right.astype(jnp.bfloat16))


def to_pair(mixed, ready, mid_gain, out_weight, out_gate):
    scaled = unit_channels(mixed.astype(jnp.float32), mid_gain).astype(jnp.bfloat16)
    scaled = lax.optimization_barrier(scaled)
    gate = jax.nn.sigmoid(
        jnp.einsum("ijc,cd->ijd", ready, out_gate, preferred_element_type=jnp.float32)
    )
    return (
        jnp.einsum("ijd,dc->ijc", scaled, out_weight, preferred_element_type=jnp.float32) * gate
    ).astype(jnp.bfloat16)


def on_device(
    pair_array, left_weight, right_weight, left_gate, right_gate, mid_gain, out_weight, out_gate
):
    ready, left, right = make_factors(pair_array, left_weight, right_weight, left_gate, right_gate)
    count = pair_array.shape[0] * lax.axis_size("pr")
    left_lines, right_lines = (
        lax.all_to_all(left, "pr", split_axis=2, concat_axis=0, tiled=True),
        lax.all_to_all(right, "pr", split_axis=2, concat_axis=0, tiled=True),
    )
    strip = jnp.einsum(
        "kid,kjd->ijd",
        lax.all_gather(left_lines, "pc", axis=1, tiled=True),
        right_lines,
        preferred_element_type=jnp.float32,
    )
    strip = (strip * count ** (-0.5)).astype(jnp.bfloat16)
    mixed = lax.all_to_all(strip, "pr", split_axis=0, concat_axis=2, tiled=True)
    return to_pair(mixed, ready, mid_gain, out_weight, out_gate)


def solution(mesh):
    return jax.shard_map(
        on_device,
        mesh=mesh,
        in_specs=(P("pr", "pc", None), P(), P(), P(), P(), P(), P(), P()),
        out_specs=P("pr", "pc", None),
        check_vma=False,
    )
```

profile of v0, /device:TPU:0, one launch (start us, length us, event | category | flops | bytes accessed | tf_op | source)
XLA Modules:
  0.0 104.0 jit_solution(1541400130074911763)
XLA Ops:
  6.5 1.0 copy-done
  7.6 1.0 fusion.24
  8.6 1.2 %fusion.14 = bf16[32,64,128]{2,1,0:T(8,128)(2,1)S(1)} fusion(f32[32,64,128]{2,1,0:T(8,128)S(1)} %fusion.24, bf16[32,64,128]{2,1,0:T(8,128)(2,1)S(1)} %copy-done, bf16[128,128]{1,0:T(8,128)(2,1)} %param.11), kind=kOutput, calls=%fused_computation.22 | convolution fusion | flops 68419584 | bytes 2129920 | tf_op jit(solution)/shard_map/ijc,cd->ijd/dot_general | solution.py:19
  9.8 1.6 %copy.25 = bf16[32,64,128]{1,0,2:T(8,128)(2,1)S(1)} copy(bf16[32,64,128]{2,1,0:T(8,128)(2,1)S(1)} %fusion.14) | data formatting | bytes 1048576 | tf_op jit(solution)/shard_map/convert_element_type | solution.py:25
  11.4 0.7 reshape.28
  12.2 14.7 %all_to_all.45 = bf16[8,2,16384]{2,1,0:T(2,128)(2,1)S(1)} all-to-all(bf16[8,2,16384]{2,1,0:T(2,128)(2,1)S(1)} %reshape.28), channel_id=1, replica_groups=mesh['pr'=8,'pc'=4] {'pr'}, dimensions={0} | all-to-all | bytes 1048576 | tf_op jit(solution)/shard_map/all_to_all | solution.py:45
  26.8 0.7 reshape.29
  27.5 0.4 copy.27
  28.0 1.6 %copy.28 = bf16[256,64,16]{0,1,2:T(8,128)(2,1)} copy(bf16[256,64,16]{1,2,0:T(8,128)(2,1)S(1)} %bitcast.66) | data formatting | bytes 1048576 | tf_op jit(solution)/shard_map/all_to_all | solution.py:45
  29.9 0.4 fusion.15
  30.4 1.6 %copy.22 = bf16[32,64,128]{1,0,2:T(8,128)(2,1)S(1)} copy(bf16[32,64,128]{2,1,0:T(8,128)(2,1)S(1)} %fusion.15) | data formatting | bytes 1048576 | tf_op jit(solution)/shard_map/convert_element_type | solution.py:25
  32.0 0.7 reshape.30
  32.7 12.1 %all_to_all.46 = bf16[8,2,16384]{2,1,0:T(2,128)(2,1)S(1)} all-to-all(bf16[8,2,16384]{2,1,0:T(2,128)(2,1)S(1)} %reshape.30), channel_id=1, replica_groups=mesh['pr'=8,'pc'=4] {'pr'}, dimensions={0} | all-to-all | bytes 1048576 | tf_op jit(solution)/shard_map/all_to_all | solution.py:46
  44.8 0.7 reshape.31
  45.9 28.9 %all-gather.2.cloned.1.call-done = bf16[256,256,16]{0,1,2:T(8,128)(2,1)} async-done(((bf16[256,64,16]{0,1,2:T(8,128)(2,1)}), bf16[256,256,16]{0,1,2:T(8,128)(2,1)}) %all-gather.2.cloned.1.call-update) | async-done | bytes 2097168 | tf_op jit(solution)/shard_map/all_gather | solution.py:50
  74.8 2.4 %fusion.18 = bf16[256,64,16]{0,1,2:T(8,128)(2,1)S(1)} fusion(bf16[256,256,16]{0,1,2:T(8,128)(2,1)} %all-gather.2.cloned.1.call-done, bf16[256,64,16]{1,2,0:T(8,128)(2,1)S(1)} %bitcast.61), kind=kOutput, calls=%fused_computation.26 | convolution fusion | flops 134742016 | bytes 3145728 | tf_op jit(solution)/shard_map/kid,kjd->ijd/dot_general | solution.py:48
  77.2 1.0 copy.30
  78.1 1.5 %reshape.32 = bf16[8,2,16384]{2,1,0:T(2,128)(2,1)} reshape(bf16[256,16,64]{2,1,0:T(8,128)(2,1)S(1)} %bitcast.64) | data formatting | bytes 1048576
  79.6 3.7 %all-to-all-start.2 = ((bf16[8,2,16384]{2,1,0:T(2,128)(2,1)}), bf16[8,2,16384]{2,1,0:T(2,128)(2,1)S(1)}, u32[]{:S(2)}, u32[]{:S(2)}) async-start(bf16[8,2,16384]{2,1,0:T(2,128)(2,1)} %reshape.32), calls=%async_computation.2 | async-start | bytes 1048576 | tf_op jit(solution)/shard_map/all_to_all | solution.py:55
  83.3 0.4 fusion.13
  83.8 9.3 %all-to-all-done.2 = bf16[8,2,16384]{2,1,0:T(2,128)(2,1)S(1)} async-done(((bf16[8,2,16384]{2,1,0:T(2,128)(2,1)}), bf16[8,2,16384]{2,1,0:T(2,128)(2,1)S(1)}, u32[]{:S(2)}, u32[]{:S(2)}) %all-to-all-start.2) | async-done | bytes 524320 | tf_op jit(solution)/shard_map/all_to_all | solution.py:55
  93.0 0.7 reshape.33
  95.2 0.5 fusion.2
  95.9 1.3 %fusion.17 = bf16[32,64,128]{2,1,0:T(8,128)(2,1)} fusion(f32[32,64,128]{2,1,0:T(8,128)S(1)} %fusion.13, bf16[32,64,128]{1,2,0:T(8,128)(2,1)S(1)} %fusion.2, bf16[128,128]{1,0:T(8,128)(2,1)S(1)} %copy-done.2), kind=kOutput, calls=%fused_computation.25 | convolution fusion | flops 67633152 | bytes 2129920 | tf_op jit(solution)/shard_map/ijd,dc->ijc/dot_general | solution.py:35
  (21 shorter events, 2.5 us)
Async XLA Ops:
  6.5 1.0 %copy-start = (bf16[32,64,128]{2,1,0:T(8,128)(2,1)S(1)}, bf16[32,64,128]{2,1,0:T(8,128)(2,1)}, u32[]{:S(2)}) copy-start(bf16[32,64,128]{2,1,0:T(8,128)(2,1)} %param.8) | copy-start | bytes 1572868
  6.5 68.3 %all-gather.2.cloned.1.call-start = ((), (), s32[]{:S(2)}) async-start(), calls=%async_computation.3 | async-start | bytes 2621440 | tf_op jit(solution)/shard_map/all_gather | solution.py:50
  27.5 2.1 %copy-start.1 = (bf16[128,128]{1,0:T(8,128)(2,1)S(1)}, bf16[128,128]{1,0:T(8,128)(2,1)}, u32[]{:S(2)}) copy-start(bf16[128,128]{1,0:T(8,128)(2,1)} %param.10) | copy-start | bytes 98308
  27.9 2.0 %copy-start.4 = (bf16[128,128]{1,0:T(8,128)(2,1)S(1)}, bf16[128,128]{1,0:T(8,128)(2,1)}, u32[]{:S(2)}) copy-start(bf16[128,128]{1,0:T(8,128)(2,1)} %param.12) | copy-start | bytes 98308
  77.2 6.2 %copy-start.5 = (bf16[128,128]{1,0:T(8,128)(2,1)S(1)}, bf16[128,128]{1,0:T(8,128)(2,1)}, u32[]{:S(2)}) copy-start(bf16[128,128]{1,0:T(8,128)(2,1)} %param.15) | copy-start | bytes 98308
  79.6 13.4 %all-to-all-start.2 = ((bf16[8,2,16384]{2,1,0:T(2,128)(2,1)}), bf16[8,2,16384]{2,1,0:T(2,128)(2,1)S(1)}, u32[]{:S(2)}, u32[]{:S(2)}) async-start(bf16[8,2,16384]{2,1,0:T(2,128)(2,1)} %reshape.32), calls=%async_computation.2 | async-start | bytes 1048576 | tf_op jit(solution)/shard_map/all_to_all | solution.py:55
  94.5 0.7 copy-start.3
  95.2 0.8 copy-start.2
Sparse Core Ops, SparseCore 0:
  29.7 45.0 all-gather.1
where the time goes:
time: 105 us; the launch traced here: 104 us
  waiting for transfers between devices  38.2 us (36%)
  blocking collectives  26.8 us (26%)
  between operations  13.6 us (13%)
  local copies, waits for them, and re-layouts  13.5 us (13%)
  matrix products  6.96 us (7%)
  starting transfers between devices  3.68 us (4%)
  other arithmetic  1.27 us (1%)
    all_gather x1, waiting for transfers between devices, on_device(): lax.all_gather(left_lines, 'pc', axis=1, tiled=True)  28.9 us
    all_to_all x1, blocking collectives, on_device(): lax.all_to_all(left, 'pr', split_axis=2, concat_axis=0, tiled=True)  14.7 us
    all_to_all x1, blocking collectives, on_device(): lax.all_to_all(right, 'pr', split_axis=2, concat_axis=0, tiled=True)  12.1 us
    all_to_all x1, waiting for transfers between devices, on_device(): mixed = lax.all_to_all(strip, 'pr', split_axis=0, concat_axis=2, tiled=True)  9.25 us
    unnamed x18, local copies, waits for them, and re-layouts  6.59 us
    all_to_all x1, starting transfers between devices, on_device(): mixed = lax.all_to_all(strip, 'pr', split_axis=0, concat_axis=2, tiled=True)  3.67 us
    convert_element_type x2, local copies, waits for them, and re-layouts, make_factors(): return (pair_in, left.astype(jnp.bfloat16), right.astype(jnp.bfloat16))  3.24 us
    dot_general x1, matrix products, on_device(): jnp.einsum('kid,kjd->ijd', lax.all_gather(left_lines, 'pc', axis=1, tiled...  2.35 us
  transfers between devices with their start and end apart: 2, of which 2 were waited for; matrix products, arithmetic and copies ran while one was open for 4% of the time, Pallas kernels for 0%

commit v1 on v0

--- a/solution.py
+++ b/solution.py
@@ -2,6 +2,12 @@
 import jax.numpy as jnp
 from jax import lax
 from jax.sharding import PartitionSpec as P
+
+
+def watch_the_matrix(vals, array_axis):
+    inter = list(vals.shape[1:])
+    inter[array_axis] *= vals.shape[0]
+    return jnp.moveaxis(vals, 0, array_axis).reshape(inter)
 
 
 def unit_channels(values, channel_gain):
@@ -45,12 +51,28 @@
         lax.all_to_all(left, "pr", split_axis=2, concat_axis=0, tiled=True),
         lax.all_to_all(right, "pr", split_axis=2, concat_axis=0, tiled=True),
     )
-    strip = jnp.einsum(
-        "kid,kjd->ijd",
-        lax.all_gather(left_lines, "pc", axis=1, tiled=True),
-        right_lines,
-        preferred_element_type=jnp.float32,
-    )
+    z2 = jax.lax.psum(1, "pc")
+    last = jax.lax.axis_index("pc")
+    out_arr, back, kept_arr = (z2, last, left_lines.shape[1])
+    sheets = [(tick, (tick + 1) % out_arr) for tick in range(out_arr)]
+    cards = [(tick, (tick - 1) % out_arr) for tick in range(out_arr)]
+    even = out_arr // 2
+    state_next = {}
+    far_arr = b_now = left_lines
+    for w in range(even + 1):
+        d_next = jax.lax.ppermute(far_arr, "pc", sheets) if w < even else None
+        shaped = jax.lax.ppermute(b_now, "pc", cards) if w < out_arr - even - 1 else None
+        state_next[-w] = jnp.einsum(
+            "kid,kjd->ijd", far_arr, right_lines, preferred_element_type=jnp.float32
+        )
+        if 0 < w < out_arr - even:
+            state_next[w] = jnp.einsum(
+                "kid,kjd->ijd", b_now, right_lines, preferred_element_type=jnp.float32
+            )
+        far_arr, b_now = (d_next, shaped)
+    state_next = jnp.stack([state_next[k] for k in sorted(state_next)], axis=0)
+    state_next = state_next[(jnp.arange(out_arr) - back + even) % out_arr]
+    strip = watch_the_matrix(state_next, 0)
     strip = (strip * count ** (-0.5)).astype(jnp.bfloat16)
     mixed = lax.all_to_all(strip, "pr", split_axis=0, concat_axis=2, tiled=True)
     return to_pair(mixed, ready, mid_gain, out_weight, out_gate)

time: 105 us -> 89.2 us (0.85)
  blocking collectives: 26.8 us -> 0 us
  between operations: 13.6 us -> 0.23 us
  starting transfers between devices: 3.68 us -> 16.4 us
  local copies, waits for them, and re-layouts: 13.5 us -> 18.4 us
  matrix products: 6.96 us -> 11 us
  other arithmetic: 1.27 us -> 4.07 us
    all_gather x1 -> x0, waiting for transfers between devices: 28.9 us -> none  [on_device(): lax.all_gather(left_lines, 'pc', axis=1, tiled=True)]
    all_to_all x2 -> x0, blocking collectives: 26.8 us -> none  [the longest x1 14.7 us: on_device(): lax.all_to_all(left, 'pr', split_axis=2, concat_axis=0, tiled=True)]
    all_to_all x0 -> x2, waiting for transfers between devices: none -> 14.6 us  [the longest x1 8.47 us: on_device(): lax.all_to_all(left, 'pr', split_axis=2, concat_axis=0, tiled=True)]
    ppermute x0 -> x3, waiting for transfers between devices: none -> 14.3 us  [the longest x2 12.8 us: on_device(): d_next = jax.lax.ppermute(far_arr, 'pc', sheets) if w < even else None]
    all_to_all x0 -> x2, starting transfers between devices: none -> 8.68 us  [the longest x1 5.18 us: on_device(): lax.all_to_all(left, 'pr', split_axis=2, concat_axis=0, tiled=True)]
    ppermute x0 -> x3, starting transfers between devices: none -> 3.92 us  [the longest x1 2.29 us: on_device(): jax.lax.ppermute(b_now, 'pc', cards)]
    gather x0 -> x1, local copies, waits for them, and re-layouts: none -> 2.27 us  [on_device(): state_next = state_next[(jnp.arange(out_arr) - back + even) % out_arr]]
    dot_general x1 -> x4, matrix products: 2.35 us -> 4.23 us  [the longest x3 2.91 us: on_device(): jnp.einsum('kid,kjd->ijd', far_arr, right_lines, preferred_element_type=j...]
  transfers between devices with their start and end apart: 2 -> 6, of which waited for: 2 -> 6; matrix products, arithmetic and copies ran while one was open for 4% -> 13% of each run, Pallas kernels for 0% -> 0%
where the time goes in v1:
time: 89.2 us; the launch traced here: 88.4 us
  waiting for transfers between devices  38.2 us (43%)
  local copies, waits for them, and re-layouts  18.4 us (21%)
  starting transfers between devices  16.4 us (18%)
  matrix products  11 us (12%)
  other arithmetic  4.07 us (5%)
    ppermute x2, waiting for transfers between devices, on_device(): d_next = jax.lax.ppermute(far_arr, 'pc', sheets) if w < even else None  12.8 us
    all_to_all x1, waiting for transfers between devices, on_device(): mixed = lax.all_to_all(strip, 'pr', split_axis=0, concat_axis=2, tiled=True)  9.28 us
    all_to_all x1, waiting for transfers between devices, on_device(): lax.all_to_all(left, 'pr', split_axis=2, concat_axis=0, tiled=True)  8.47 us
    unnamed x18, local copies, waits for them, and re-layouts  8.19 us
    all_to_all x1, waiting for transfers between devices, on_device(): lax.all_to_all(right, 'pr', split_axis=2, concat_axis=0, tiled=True)  6.09 us
    all_to_all x1, starting transfers between devices, on_device(): lax.all_to_all(left, 'pr', split_axis=2, concat_axis=0, tiled=True)  5.18 us
    all_to_all x1, starting transfers between devices, on_device(): mixed = lax.all_to_all(strip, 'pr', split_axis=0, concat_axis=2, tiled=True)  3.85 us
    all_to_all x1, starting transfers between devices, on_device(): lax.all_to_all(right, 'pr', split_axis=2, concat_axis=0, tiled=True)  3.49 us
  transfers between devices with their start and end apart: 6, of which 6 were waited for; matrix products, arithmetic and copies ran while one was open for 13% of the time, Pallas kernels for 0%

profile of v1, /device:TPU:0, one launch (start us, length us, event | category | flops | bytes accessed | tf_op | source)
XLA Modules:
  0.0 88.4 jit_solution(1121825788342698668)
XLA Ops:
  3.3 1.6 %copy.47 = bf16[32,64,128]{1,0,2:T(8,128)(2,1)S(1)} copy(bf16[32,64,128]{2,1,0:T(8,128)(2,1)S(1)} %fusion.14) | data formatting | bytes 1048576 | tf_op jit(solution)/shard_map/convert_element_type | solution.py:31
  4.9 1.5 %reshape.94 = bf16[8,2,16384]{2,1,0:T(2,128)(2,1)} reshape(bf16[128,32,64]{2,1,0:T(8,128)(2,1)S(1)} %bitcast.85) | data formatting | bytes 1048576
  6.4 5.2 %all-to-all-start.1 = ((bf16[8,2,16384]{2,1,0:T(2,128)(2,1)}), bf16[8,2,16384]{2,1,0:T(2,128)(2,1)S(1)}, u32[]{:S(2)}, u32[]{:S(2)}) async-start(bf16[8,2,16384]{2,1,0:T(2,128)(2,1)} %reshape.94), calls=%async_computation.1 | async-start | bytes 1048576 | tf_op jit(solution)/shard_map/all_to_all | solution.py:51
  11.6 1.2 %fusion.24 = f32[32,64,128]{2,1,0:T(8,128)} fusion(bf16[32,64,128]{2,1,0:T(8,128)(2,1)S(1)} %copy-done, bf16[128,128]{1,0:T(8,128)(2,1)S(1)} %copy-done.1), kind=kOutput, calls=%fused_computation.38 | convolution fusion | flops 67108864 | bytes 1605632 | tf_op jit(solution)/shard_map/ijc,cd->ijd/dot_general | solution.py:27
  12.9 8.5 %all-to-all-done.1 = bf16[8,2,16384]{2,1,0:T(2,128)(2,1)S(1)} async-done(((bf16[8,2,16384]{2,1,0:T(2,128)(2,1)}), bf16[8,2,16384]{2,1,0:T(2,128)(2,1)S(1)}, u32[]{:S(2)}, u32[]{:S(2)}) %all-to-all-start.1) | async-done | bytes 524320 | tf_op jit(solution)/shard_map/all_to_all | solution.py:51
  23.3 1.6 %collective-permute-start = (bf16[256,64,16]{0,1,2:T(8,128)(2,1)S(1)}, bf16[256,64,16]{0,1,2:T(8,128)(2,1)}, u32[]{:S(2)}, u32[]{:S(2)}) collective-permute-start(bf16[256,64,16]{0,1,2:T(8,128)(2,1)S(1)} %copy.50), channel_id=1, source_target_pairs={{0,1},{1,2},{2,3},{3,0},{4,5},{5,6},{6,7},{7,4},{8,9},{9,10},{10,1... | collective-permute-start | bytes 1572872 | tf_op jit(solution)/shard_map/ppermute | solution.py:63
  24.9 1.7 %fusion.15 = bf16[32,64,128]{2,1,0:T(8,128)(2,1)S(1)} fusion(f32[32,64,128]{2,1,0:T(8,128)} %fusion.24, bf16[32,64,128]{2,1,0:T(8,128)(2,1)S(1)} %copy-done, bf16[128,128]{1,0:T(8,128)(2,1)S(1)} %copy-done.4), kind=kOutput, calls=%fused_computation.25 | convolution fusion | flops 68419584 | bytes 2129920 | tf_op jit(solution)/shard_map/ijc,cd->ijd/dot_general | solution.py:29
  26.6 1.6 %copy.44 = bf16[32,64,128]{1,0,2:T(8,128)(2,1)S(1)} copy(bf16[32,64,128]{2,1,0:T(8,128)(2,1)S(1)} %fusion.15) | data formatting | bytes 1048576 | tf_op jit(solution)/shard_map/convert_element_type | solution.py:31
  28.2 1.5 %reshape.92 = bf16[8,2,16384]{2,1,0:T(2,128)(2,1)} reshape(bf16[128,32,64]{2,1,0:T(8,128)(2,1)S(1)} %bitcast.86) | data formatting | bytes 1048576
  29.7 3.5 %all-to-all-start = ((bf16[8,2,16384]{2,1,0:T(2,128)(2,1)}), bf16[8,2,16384]{2,1,0:T(2,128)(2,1)S(1)}, u32[]{:S(2)}, u32[]{:S(2)}) async-start(bf16[8,2,16384]{2,1,0:T(2,128)(2,1)} %reshape.92), calls=%async_computation | async-start | bytes 1048576 | tf_op jit(solution)/shard_map/all_to_all | solution.py:52
  33.2 2.3 %collective-permute-start.2 = (bf16[256,64,16]{0,1,2:T(8,128)(2,1)S(1)}, bf16[256,64,16]{0,1,2:T(8,128)(2,1)}, u32[]{:S(2)}, u32[]{:S(2)}) collective-permute-start(bf16[256,64,16]{0,1,2:T(8,128)(2,1)S(1)} %copy.50), channel_id=1, source_target_pairs={{0,3},{1,0},{2,1},{3,2},{4,7},{5,4},{6,5},{7,6},{8,11},{9,8},{10,9... | collective-permute-start | bytes 1572872 | tf_op jit(solution)/shard_map/ppermute | solution.py:64
  36.7 6.1 %all-to-all-done = bf16[8,2,16384]{2,1,0:T(2,128)(2,1)S(1)} async-done(((bf16[8,2,16384]{2,1,0:T(2,128)(2,1)}), bf16[8,2,16384]{2,1,0:T(2,128)(2,1)S(1)}, u32[]{:S(2)}, u32[]{:S(2)}) %all-to-all-start) | async-done | bytes 524320 | tf_op jit(solution)/shard_map/all_to_all | solution.py:52
  45.0 1.3 %convolution_bitcast_fusion.2 = f32[1,64,64,16]{1,2,3,0:T(8,128)S(1)} fusion(bf16[256,64,16]{0,1,2:T(8,128)(2,1)S(1)} %copy.51, bf16[256,64,16]{0,1,2:T(8,128)(2,1)} %collective-permute-done), kind=kOutput, calls=%fused_computation.29 | convolution fusion | flops 33554432 | bytes 1310720 | tf_op jit(solution)/shard_map/kid,kjd->ijd/dot_general | solution.py:65
  46.4 1.6 %collective-permute-done.2 = bf16[256,64,16]{0,1,2:T(8,128)(2,1)} collective-permute-done((bf16[256,64,16]{0,1,2:T(8,128)(2,1)S(1)}, bf16[256,64,16]{0,1,2:T(8,128)(2,1)}, u32[]{:S(2)}, u32[]{:S(2)}) %collective-permute-start.2) | collective-permute-done | bytes 524320 | tf_op jit(solution)/shard_map/ppermute | solution.py:64
  47.9 1.3 %convolution_bitcast_fusion = f32[1,64,64,16]{1,2,3,0:T(8,128)S(1)} fusion(bf16[256,64,16]{0,1,2:T(8,128)(2,1)S(1)} %copy.51, bf16[256,64,16]{0,1,2:T(8,128)(2,1)} %collective-permute-done.2), kind=kOutput, calls=%fused_computation.27 | convolution fusion | flops 33554432 | bytes 1310720 | tf_op jit(solution)/shard_map/kid,kjd->ijd/dot_general | solution.py:69
  49.3 11.5 %collective-permute-done.1 = bf16[256,64,16]{0,1,2:T(8,128)(2,1)} collective-permute-done((bf16[256,64,16]{0,1,2:T(8,128)(2,1)}, bf16[256,64,16]{0,1,2:T(8,128)(2,1)}, u32[]{:S(2)}, u32[]{:S(2)}) %collective-permute-start.1) | collective-permute-done | bytes 524320 | tf_op jit(solution)/shard_map/ppermute | solution.py:63
  60.8 1.3 %convolution_bitcast_fusion.3 = f32[1,64,64,16]{1,2,3,0:T(8,128)S(1)} fusion(bf16[256,64,16]{0,1,2:T(8,128)(2,1)S(1)} %copy.51, bf16[256,64,16]{0,1,2:T(8,128)(2,1)} %collective-permute-done.1), kind=kOutput, calls=%fused_computation.30 | convolution fusion | flops 33554432 | bytes 1310720 | tf_op jit(solution)/shard_map/kid,kjd->ijd/dot_general | solution.py:65
  62.1 1.5 %pad_maximum_fusion = f32[4,64,64,16]{1,2,3,0:T(8,128)} fusion(f32[1,64,64,16]{1,2,3,0:T(8,128)S(1)} %convolution_bitcast_fusion, f32[1,64,64,16]{1,2,3,0:T(8,128)S(1)} %convolution_bitcast_fusion.1, f32[1,64,64,16]{1,2,3,0:T(8,128)S(1)} %convolution_bitcast_fusion.2, f32[1,64,64,16]{1,2,3,0:T(8,128)S(1)} %convolution_bitcast_fusion.3), kind=kLoop, calls=%fused_computation.1 | loop fusion | flops 786432 | bytes 2097152 | tf_op jit(solution)/shard_map/stack | solution.py:73
  63.7 2.3 %gather_fusion = f32[4,64,64,16]{1,2,3,0:T(8,128)S(1)} fusion(f32[4,64,64,16]{1,2,3,0:T(8,128)} %pad_maximum_fusion, s32[1024]{0:T(1024)S(1)} %pad_clamp_fusion), kind=kCustom, calls=%fused_computation | custom fusion | bytes 2097168 | tf_op jit(solution)/shard_map/gather | solution.py:74
  67.2 1.9 %copy.64 = bf16[4,64,64,16]{2,3,1,0:T(8,128)(2,1)S(1)} copy(bf16[4,64,64,16]{1,2,3,0:T(8,128)(2,1)} %multiply_convert_fusion) | data formatting | bytes 1048576 | tf_op jit(solution)/shard_map/convert_element_type | solution.py:76
  69.1 1.5 %reshape.96 = bf16[8,2,16384]{2,1,0:T(2,128)(2,1)} reshape(bf16[256,16,64]{2,1,0:T(8,128)(2,1)S(1)} %bitcast.91) | data formatting | bytes 1048576
  70.6 3.8 %all-to-all-start.2 = ((bf16[8,2,16384]{2,1,0:T(2,128)(2,1)}), bf16[8,2,16384]{2,1,0:T(2,128)(2,1)S(1)}, u32[]{:S(2)}, u32[]{:S(2)}) async-start(bf16[8,2,16384]{2,1,0:T(2,128)(2,1)} %reshape.96), calls=%async_computation.2 | async-start | bytes 1048576 | tf_op jit(solution)/shard_map/all_to_all | solution.py:77
  74.9 9.3 %all-to-all-done.2 = bf16[8,2,16384]{2,1,0:T(2,128)(2,1)S(1)} async-done(((bf16[8,2,16384]{2,1,0:T(2,128)(2,1)}), bf16[8,2,16384]{2,1,0:T(2,128)(2,1)S(1)}, u32[]{:S(2)}, u32[]{:S(2)}) %all-to-all-start.2) | async-done | bytes 524320 | tf_op jit(solution)/shard_map/all_to_all | solution.py:77
  87.1 1.3 %fusion.16 = bf16[32,64,128]{2,1,0:T(8,128)(2,1)} fusion(f32[32,64,128]{2,1,0:T(8,128)S(1)} %fusion.13, bf16[32,64,128]{1,2,0:T(8,128)(2,1)S(1)} %fusion.2, bf16[128,128]{1,0:T(8,128)(2,1)S(1)} %copy-done.2), kind=kOutput, calls=%fused_computation.26 | convolution fusion | flops 67633152 | bytes 2129920 | tf_op jit(solution)/shard_map/ijd,dc->ijc/dot_general | solution.py:41
  (35 shorter events, 13.1 us)
Async XLA Ops:
  0.0 1.0 %copy-start = (bf16[32,64,128]{2,1,0:T(8,128)(2,1)S(1)}, bf16[32,64,128]{2,1,0:T(8,128)(2,1)}, u32[]{:S(2)}) copy-start(bf16[32,64,128]{2,1,0:T(8,128)(2,1)} %param.8) | copy-start | bytes 1572868
  3.3 8.3 %copy-start.1 = (bf16[128,128]{1,0:T(8,128)(2,1)S(1)}, bf16[128,128]{1,0:T(8,128)(2,1)}, u32[]{:S(2)}) copy-start(bf16[128,128]{1,0:T(8,128)(2,1)} %param.10) | copy-start | bytes 98308
  6.4 14.9 %all-to-all-start.1 = ((bf16[8,2,16384]{2,1,0:T(2,128)(2,1)}), bf16[8,2,16384]{2,1,0:T(2,128)(2,1)S(1)}, u32[]{:S(2)}, u32[]{:S(2)}) async-start(bf16[8,2,16384]{2,1,0:T(2,128)(2,1)} %reshape.94), calls=%async_computation.1 | async-start | bytes 1048576 | tf_op jit(solution)/shard_map/all_to_all | solution.py:51
  22.0 2.9 %copy-start.4 = (bf16[128,128]{1,0:T(8,128)(2,1)S(1)}, bf16[128,128]{1,0:T(8,128)(2,1)}, u32[]{:S(2)}) copy-start(bf16[128,128]{1,0:T(8,128)(2,1)} %param.12) | copy-start | bytes 98308
  23.3 13.5 %collective-permute-start = (bf16[256,64,16]{0,1,2:T(8,128)(2,1)S(1)}, bf16[256,64,16]{0,1,2:T(8,128)(2,1)}, u32[]{:S(2)}, u32[]{:S(2)}) collective-permute-start(bf16[256,64,16]{0,1,2:T(8,128)(2,1)S(1)} %copy.50), channel_id=1, source_target_pairs={{0,1},{1,2},{2,3},{3,0},{4,5},{5,6},{6,7},{7,4},{8,9},{9,10},{10,1... | collective-permute-start | bytes 1572872 | tf_op jit(solution)/shard_map/ppermute | solution.py:63
  29.7 13.2 %all-to-all-start = ((bf16[8,2,16384]{2,1,0:T(2,128)(2,1)}), bf16[8,2,16384]{2,1,0:T(2,128)(2,1)S(1)}, u32[]{:S(2)}, u32[]{:S(2)}) async-start(bf16[8,2,16384]{2,1,0:T(2,128)(2,1)} %reshape.92), calls=%async_computation | async-start | bytes 1048576 | tf_op jit(solution)/shard_map/all_to_all | solution.py:52
  33.2 14.7 %collective-permute-start.2 = (bf16[256,64,16]{0,1,2:T(8,128)(2,1)S(1)}, bf16[256,64,16]{0,1,2:T(8,128)(2,1)}, u32[]{:S(2)}, u32[]{:S(2)}) collective-permute-start(bf16[256,64,16]{0,1,2:T(8,128)(2,1)S(1)} %copy.50), channel_id=1, source_target_pairs={{0,3},{1,0},{2,1},{3,2},{4,7},{5,4},{6,5},{7,6},{8,11},{9,8},{10,9... | collective-permute-start | bytes 1572872 | tf_op jit(solution)/shard_map/ppermute | solution.py:64
  36.7 24.1 %collective-permute-start.1 = (bf16[256,64,16]{0,1,2:T(8,128)(2,1)}, bf16[256,64,16]{0,1,2:T(8,128)(2,1)}, u32[]{:S(2)}, u32[]{:S(2)}) collective-permute-start(bf16[256,64,16]{0,1,2:T(8,128)(2,1)} %collective-permute-done), channel_id=1, source_target_pairs={{0,1},{1,2},{2,3},{3,0},{4,5},{5,6},{6,7},{7,4},{8,9},{9,10},{10,1... | collective-permute-start | bytes 1572872 | tf_op jit(solution)/shard_map/ppermute | solution.py:63
  67.2 7.3 %copy-start.5 = (bf16[128,128]{1,0:T(8,128)(2,1)S(1)}, bf16[128,128]{1,0:T(8,128)(2,1)}, u32[]{:S(2)}) copy-start(bf16[128,128]{1,0:T(8,128)(2,1)} %param.15) | copy-start | bytes 98308
  70.6 13.6 %all-to-all-start.2 = ((bf16[8,2,16384]{2,1,0:T(2,128)(2,1)}), bf16[8,2,16384]{2,1,0:T(2,128)(2,1)S(1)}, u32[]{:S(2)}, u32[]{:S(2)}) async-start(bf16[8,2,16384]{2,1,0:T(2,128)(2,1)} %reshape.96), calls=%async_computation.2 | async-start | bytes 1048576 | tf_op jit(solution)/shard_map/all_to_all | solution.py:77
  85.7 0.7 copy-start.3
  86.3 0.8 copy-start.2
